TPU v7x, 256 devices: a whole 4x4x8 slice. The times are simulated.
256 devices in a mesh: blk: 128 (over y, z, x), grp: 2 (over core).
Axes of the slice: x: 4, y: 4, z: 8, core: 2. Of those that a mesh axis runs over, the one named last changes fastest.
Arguments:
- schur_blocks: bfloat16 [512, 1024, 1024], P(('blk', 'grp')), may hold values from -1 to 5, as said below
- residual: float32 [512, 1024, 128], P(('blk', 'grp')), may hold values from -200 to 200
- direction: float32 [512, 1024, 128], P(('blk', 'grp')), may hold values from -200 to 200
- corner_map: int32 [512, 24], P(('blk', 'grp')), may hold values from 0 to 63
- panel_order: int32 [8], replicated, may hold values from 0 to 7, each once
- coarse_factor: float32 [8, 8, 1024, 1024], P(None, None, 'blk'), may hold values from -0.0625 to 0.0625
- block_inverses: float32 [8, 1024, 1024], P(None, 'blk'), may hold values from -0.1875 to 0.1875
Outputs:
- residual_next: float32 [512, 1024, 128], P(('blk', 'grp'))
- direction_next: float32 [512, 1024, 128], P(('blk', 'grp'))
Inputs may be any that keep to these rules, and one draw needn't show every extreme that they name: `schur_blocks`: each subdomain's block is symmetric positive definite. `panel_order`: each coarse block appears once.
All inputs are finite; a program needn't handle non-finite values.
Results may differ from a plain program's by a relative error of at most 0.0048.
Values sent between devices are 32-bit elements; how exact they have to be, the bound alone decides.
A program may use at most 64 MiB of HBM per device.

v0:
```python
import functools

import jax
import jax.numpy as jnp
from jax import lax
from jax.sharding import Mesh
from jax.sharding import PartitionSpec as P

PANELS = 8
BLK_GRP = ("blk_0", "blk_1", "blk_2", "grp")
BLK = ("blk_0", "blk_1", "blk_2")


precise = lax.Precision.HIGHEST


def one_axis_at_a_time(shard, axes):
    return functools.reduce(lax.psum, axes, shard)


def copy_for_each(shard, axis):
    copies = jnp.broadcast_to(shard, (lax.axis_size(axis), *shard.shape))
    return lax.all_to_all(copies, axis, split_axis=0, concat_axis=0, tiled=True)


def in_order(tiles, dim):
    tiles = jnp.moveaxis(tiles, 0, dim)
    shape = tiles.shape
    return tiles.reshape(*shape[:dim], shape[dim] * shape[dim + 1], *shape[dim + 2 :])


def whole_of(shard, axes, dim):
    far, near = axes
    tiles = copy_for_each(copy_for_each(shard, far), near)
    return in_order(tiles.swapaxes(0, 1).reshape(-1, *shard.shape), dim)


def of_everyone(shard, axis):
    return copy_for_each(shard, axis).sum(axis=0)


def squares(residual):
    return one_axis_at_a_time(jnp.sum(residual * residual, axis=(0, 1)), BLK_GRP)


def solve(coarse, panel_order, coarse_factor, block_inverses):
    pending = jnp.zeros_like(coarse)
    solved = jnp.zeros_like(coarse)
    for position in range(PANELS):
        current = panel_order[position]
        target = lax.dynamic_index_in_dim(coarse - pending, current, 0, keepdims=False)
        inverse = lax.dynamic_index_in_dim(block_inverses, current, 0, keepdims=False)
        block_value = jnp.dot(
            inverse,
            whole_of(target, (("blk_0", "blk_1"), "blk_2"), 0),
            precision=precise,
            preferred_element_type=jnp.float32,
        )
        solved = lax.dynamic_update_index_in_dim(solved, block_value, current, 0)
        if position + 1 < PANELS:
            coupling = lax.dynamic_index_in_dim(coarse_factor, current, 1, keepdims=False)
            pending = pending + jnp.einsum(
                "aic,cv->aiv",
                coupling,
                whole_of(block_value, (("blk_0", "blk_1"), "blk_2"), 0),
                precision=precise,
            )
    return solved


def local(
    schur_blocks, residual, direction, corner_map, panel_order, coarse_factor, block_inverses
):
    panels = block_inverses.shape[0]
    rows_b = block_inverses.shape[1]
    sub_count = schur_blocks.shape[0]
    corners = corner_map.shape[1]
    columns_iota = lax.broadcasted_iota(jnp.int32, (sub_count, corners, panels * rows_b), 2)
    placing = (corner_map[:, :, None] == columns_iota).astype(jnp.float32)
    norm_now = squares(residual)
    applied = jnp.einsum(
        "sij,sjv->siv",
        schur_blocks,
        direction.astype(jnp.bfloat16),
        preferred_element_type=jnp.float32,
    )
    curvature = one_axis_at_a_time(jnp.sum(direction * applied, axis=(0, 1)), BLK_GRP)
    step_size = norm_now / curvature
    residual = residual - step_size * applied
    norm_next = squares(residual)
    corner_part = jnp.einsum("scm,scv->mv", placing, residual[:, :corners, :], precision=precise)
    corner_part = corner_part.reshape(panels, rows_b, -1)
    coarse_part = of_everyone(corner_part, "grp")
    solved = solve(coarse_part, panel_order, coarse_factor, block_inverses)
    flat_solved = solved.reshape(panels * rows_b, -1)
    correction = jnp.einsum("scm,mv->scv", placing, flat_solved, precision=precise)
    corrected = jnp.concatenate(
        [residual[:, :corners, :] + correction, residual[:, corners:, :]], axis=1
    )
    direction = corrected + norm_next / norm_now * direction
    return (residual, direction)


def solution(mesh):
    split = Mesh(
        mesh.devices.reshape(4, 8, 4, mesh.shape["grp"]), ("blk_0", "blk_1", "blk_2", "grp")
    )
    placed = (
        P(BLK_GRP, None, None),
        P(BLK_GRP, None, None),
        P(BLK_GRP, None, None),
        P(BLK_GRP, None),
        P(),
        P(None, None, BLK, None),
        P(None, BLK, None),
    )
    return jax.shard_map(
        local,
        mesh=split,
        in_specs=placed,
        out_specs=(P(BLK_GRP, None, None), P(BLK_GRP, None, None)),
        check_vma=False,
    )
```

profile of v0, /device:TPU:1, one launch (start us, length us, event | category | flops | bytes accessed | tf_op | source)
XLA Modules:
  0.0 491.0 jit_solution(257068401126563207)
XLA Ops:
  0.6 1.7 multiply_reduce_fusion.2
  2.3 4.2 multiply_reduce_fusion.1
  6.5 9.5 %all-reduce.2 = (f32[128]{0:T(128)S(1)}, f32[128]{0:T(128)S(1)}) all-reduce(f32[128]{0:T(128)S(1)} %multiply_reduce_fusion.2, f32[128]{0:T(128)S(1)} %get-tuple-element.20), channel_id=1, replica_groups=mesh['blk_0'=4,'blk_1'=8,'blk_2'=4,'grp'=2] {'blk_0'}, use_global_device_ids=true, to_apply=%region_1.0 | all-reduce | flops 256 | bytes 2048 | tf_op jit(solution)/shard_map/psum | solution.py:18
  16.1 16.2 %all-reduce = (f32[128]{0:T(128)S(1)}, f32[128]{0:T(128)S(1)}) all-reduce(f32[128]{0:T(128)S(1)} %get-tuple-element.6, f32[128]{0:T(128)S(1)} %get-tuple-element.7), channel_id=1, replica_groups=mesh['blk_0'=4,'blk_1'=8,'blk_2'=4,'grp'=2] {'blk_1'}, use_global_device_ids=true, to_apply=%region_2.0 | all-reduce | flops 256 | bytes 2048 | tf_op jit(solution)/shard_map/psum | solution.py:18
  32.3 8.5 %all-reduce.1 = (f32[128]{0:T(128)S(1)}, f32[128]{0:T(128)S(1)}) all-reduce(f32[128]{0:T(128)S(1)} %get-tuple-element.2, f32[128]{0:T(128)S(1)} %get-tuple-element.3), channel_id=1, replica_groups=mesh['blk_0'=4,'blk_1'=8,'blk_2'=4,'grp'=2] {'blk_2'}, use_global_device_ids=true, to_apply=%region_3.0 | all-reduce | flops 256 | bytes 2048 | tf_op jit(solution)/shard_map/psum | solution.py:18
  40.7 10.6 %all-reduce.3 = (f32[128]{0:T(128)S(1)}, f32[128]{0:T(128)S(1)}) all-reduce(f32[128]{0:T(128)S(1)} %get-tuple-element.4, f32[128]{0:T(128)S(1)} %get-tuple-element.5), channel_id=1, replica_groups=mesh['blk_0'=4,'blk_1'=8,'blk_2'=4,'grp'=2] {'grp'}, use_global_device_ids=true, to_apply=%region_4.0 | all-reduce | flops 256 | bytes 2048 | tf_op jit(solution)/shard_map/psum | solution.py:18
  51.3 1.5 multiply_reduce_fusion
  52.9 1.0 copy-done.2
  54.1 0.6 broadcast_in_dim.125
  54.7 3.6 all-to-all-start
  58.4 0.7 fusion.77
  61.0 13.0 %all_to_all.155 = f32[32,8,128]{2,1,0:T(8,128)S(1)} all-to-all(f32[32,8,128]{2,1,0:T(8,128)S(1)} %broadcast_in_dim.126), channel_id=1, replica_groups=mesh['blk_0'=4,'blk_1'=8,'blk_2'=4,'grp'=2] {'blk_0','blk_1'}, dimensions={0} | all-to-all | bytes 262144 | tf_op jit(solution)/shard_map/all_to_all | solution.py:23
  74.0 9.6 %all_to_all.156 = f32[4,32,8,128]{3,2,1,0:T(8,128)S(1)} all-to-all(f32[4,32,8,128]{3,2,1,0:T(8,128)S(1)} %broadcast_in_dim.127), channel_id=1, replica_groups=mesh['blk_0'=4,'blk_1'=8,'blk_2'=4,'grp'=2] {'blk_2'}, dimensions={0} | all-to-all | bytes 1048576 | tf_op jit(solution)/shard_map/all_to_all | solution.py:23
  84.1 14.8 %all_to_all.157 = f32[32,8,128]{2,1,0:T(8,128)S(1)} all-to-all(f32[32,8,128]{2,1,0:T(8,128)S(1)} %broadcast_in_dim.129), channel_id=1, replica_groups=mesh['blk_0'=4,'blk_1'=8,'blk_2'=4,'grp'=2] {'blk_0','blk_1'}, dimensions={0} | all-to-all | bytes 262144 | tf_op jit(solution)/shard_map/all_to_all | solution.py:23
  98.9 0.8 broadcast_in_dim.130
  99.8 3.5 all-to-all-start.4
  105.3 4.9 all-to-all-done.4
  110.7 12.6 %all_to_all.158 = f32[32,8,128]{2,1,0:T(8,128)S(1)} all-to-all(f32[32,8,128]{2,1,0:T(8,128)S(1)} %broadcast_in_dim.131), channel_id=1, replica_groups=mesh['blk_0'=4,'blk_1'=8,'blk_2'=4,'grp'=2] {'blk_0','blk_1'}, dimensions={0} | all-to-all | bytes 262144 | tf_op jit(solution)/shard_map/all_to_all | solution.py:23
  123.4 9.3 %all_to_all.159 = f32[4,32,8,128]{3,2,1,0:T(8,128)S(1)} all-to-all(f32[4,32,8,128]{3,2,1,0:T(8,128)S(1)} %broadcast_in_dim.132), channel_id=1, replica_groups=mesh['blk_0'=4,'blk_1'=8,'blk_2'=4,'grp'=2] {'blk_2'}, dimensions={0} | all-to-all | bytes 1048576 | tf_op jit(solution)/shard_map/all_to_all | solution.py:23
  133.1 12.6 %all_to_all.160 = f32[32,8,128]{2,1,0:T(8,128)S(1)} all-to-all(f32[32,8,128]{2,1,0:T(8,128)S(1)} %broadcast_in_dim.134), channel_id=1, replica_groups=mesh['blk_0'=4,'blk_1'=8,'blk_2'=4,'grp'=2] {'blk_0','blk_1'}, dimensions={0} | all-to-all | bytes 262144 | tf_op jit(solution)/shard_map/all_to_all | solution.py:23
  145.7 0.8 broadcast_in_dim.135
  146.6 3.5 all-to-all-start.8
  151.7 5.2 %all-to-all-done.8 = f32[4,32,8,128]{3,2,1,0:T(8,128)S(1)} async-done(((f32[4,32,8,128]{3,2,1,0:T(8,128)}), f32[4,32,8,128]{3,2,1,0:T(8,128)S(1)}, u32[]{:S(2)}, u32[]{:S(2)}) %all-to-all-start.8) | async-done | bytes 524320 | tf_op jit(solution)/shard_map/all_to_all | solution.py:23
  157.5 12.4 %all_to_all.161 = f32[32,8,128]{2,1,0:T(8,128)S(1)} all-to-all(f32[32,8,128]{2,1,0:T(8,128)S(1)} %broadcast_in_dim.136), channel_id=1, replica_groups=mesh['blk_0'=4,'blk_1'=8,'blk_2'=4,'grp'=2] {'blk_0','blk_1'}, dimensions={0} | all-to-all | bytes 262144 | tf_op jit(solution)/shard_map/all_to_all | solution.py:23
  170.0 9.6 %all_to_all.162 = f32[4,32,8,128]{3,2,1,0:T(8,128)S(1)} all-to-all(f32[4,32,8,128]{3,2,1,0:T(8,128)S(1)} %broadcast_in_dim.137), channel_id=1, replica_groups=mesh['blk_0'=4,'blk_1'=8,'blk_2'=4,'grp'=2] {'blk_2'}, dimensions={0} | all-to-all | bytes 1048576 | tf_op jit(solution)/shard_map/all_to_all | solution.py:23
  180.0 12.4 %all_to_all.163 = f32[32,8,128]{2,1,0:T(8,128)S(1)} all-to-all(f32[32,8,128]{2,1,0:T(8,128)S(1)} %broadcast_in_dim.139), channel_id=1, replica_groups=mesh['blk_0'=4,'blk_1'=8,'blk_2'=4,'grp'=2] {'blk_0','blk_1'}, dimensions={0} | all-to-all | bytes 262144 | tf_op jit(solution)/shard_map/all_to_all | solution.py:23
  192.5 0.8 broadcast_in_dim.140
  193.3 3.5 all-to-all-start.12
  198.8 5.1 %all-to-all-done.12 = f32[4,32,8,128]{3,2,1,0:T(8,128)S(1)} async-done(((f32[4,32,8,128]{3,2,1,0:T(8,128)}), f32[4,32,8,128]{3,2,1,0:T(8,128)S(1)}, u32[]{:S(2)}, u32[]{:S(2)}) %all-to-all-start.12) | async-done | bytes 524320 | tf_op jit(solution)/shard_map/all_to_all | solution.py:23
  204.5 12.4 %all_to_all.164 = f32[32,8,128]{2,1,0:T(8,128)S(1)} all-to-all(f32[32,8,128]{2,1,0:T(8,128)S(1)} %broadcast_in_dim.141), channel_id=1, replica_groups=mesh['blk_0'=4,'blk_1'=8,'blk_2'=4,'grp'=2] {'blk_0','blk_1'}, dimensions={0} | all-to-all | bytes 262144 | tf_op jit(solution)/shard_map/all_to_all | solution.py:23
  217.0 9.6 %all_to_all.165 = f32[4,32,8,128]{3,2,1,0:T(8,128)S(1)} all-to-all(f32[4,32,8,128]{3,2,1,0:T(8,128)S(1)} %broadcast_in_dim.142), channel_id=1, replica_groups=mesh['blk_0'=4,'blk_1'=8,'blk_2'=4,'grp'=2] {'blk_2'}, dimensions={0} | all-to-all | bytes 1048576 | tf_op jit(solution)/shard_map/all_to_all | solution.py:23
  227.0 12.6 %all_to_all.166 = f32[32,8,128]{2,1,0:T(8,128)S(1)} all-to-all(f32[32,8,128]{2,1,0:T(8,128)S(1)} %broadcast_in_dim.144), channel_id=1, replica_groups=mesh['blk_0'=4,'blk_1'=8,'blk_2'=4,'grp'=2] {'blk_0','blk_1'}, dimensions={0} | all-to-all | bytes 262144 | tf_op jit(solution)/shard_map/all_to_all | solution.py:23
  239.6 0.8 broadcast_in_dim.145
  240.5 3.5 all-to-all-start.16
  245.6 5.2 %all-to-all-done.16 = f32[4,32,8,128]{3,2,1,0:T(8,128)S(1)} async-done(((f32[4,32,8,128]{3,2,1,0:T(8,128)}), f32[4,32,8,128]{3,2,1,0:T(8,128)S(1)}, u32[]{:S(2)}, u32[]{:S(2)}) %all-to-all-start.16) | async-done | bytes 524320 | tf_op jit(solution)/shard_map/all_to_all | solution.py:23
  251.4 12.6 %all_to_all.167 = f32[32,8,128]{2,1,0:T(8,128)S(1)} all-to-all(f32[32,8,128]{2,1,0:T(8,128)S(1)} %broadcast_in_dim.146), channel_id=1, replica_groups=mesh['blk_0'=4,'blk_1'=8,'blk_2'=4,'grp'=2] {'blk_0','blk_1'}, dimensions={0} | all-to-all | bytes 262144 | tf_op jit(solution)/shard_map/all_to_all | solution.py:23
  264.0 9.3 %all_to_all.168 = f32[4,32,8,128]{3,2,1,0:T(8,128)S(1)} all-to-all(f32[4,32,8,128]{3,2,1,0:T(8,128)S(1)} %broadcast_in_dim.147), channel_id=1, replica_groups=mesh['blk_0'=4,'blk_1'=8,'blk_2'=4,'grp'=2] {'blk_2'}, dimensions={0} | all-to-all | bytes 1048576 | tf_op jit(solution)/shard_map/all_to_all | solution.py:23
  273.8 12.5 %all_to_all.169 = f32[32,8,128]{2,1,0:T(8,128)S(1)} all-to-all(f32[32,8,128]{2,1,0:T(8,128)S(1)} %broadcast_in_dim.149), channel_id=1, replica_groups=mesh['blk_0'=4,'blk_1'=8,'blk_2'=4,'grp'=2] {'blk_0','blk_1'}, dimensions={0} | all-to-all | bytes 262144 | tf_op jit(solution)/shard_map/all_to_all | solution.py:23
  286.3 0.8 broadcast_in_dim.150
  287.2 3.5 all-to-all-start.20
  292.5 5.0 %all-to-all-done.20 = f32[4,32,8,128]{3,2,1,0:T(8,128)S(1)} async-done(((f32[4,32,8,128]{3,2,1,0:T(8,128)}), f32[4,32,8,128]{3,2,1,0:T(8,128)S(1)}, u32[]{:S(2)}, u32[]{:S(2)}) %all-to-all-start.20) | async-done | bytes 524320 | tf_op jit(solution)/shard_map/all_to_all | solution.py:23
  298.1 12.4 %all_to_all.170 = f32[32,8,128]{2,1,0:T(8,128)S(1)} all-to-all(f32[32,8,128]{2,1,0:T(8,128)S(1)} %broadcast_in_dim.151), channel_id=1, replica_groups=mesh['blk_0'=4,'blk_1'=8,'blk_2'=4,'grp'=2] {'blk_0','blk_1'}, dimensions={0} | all-to-all | bytes 262144 | tf_op jit(solution)/shard_map/all_to_all | solution.py:23
  310.5 12.1 %all_to_all.171 = f32[4,32,8,128]{3,2,1,0:T(8,128)S(1)} all-to-all(f32[4,32,8,128]{3,2,1,0:T(8,128)S(1)} %broadcast_in_dim.152), channel_id=1, replica_groups=mesh['blk_0'=4,'blk_1'=8,'blk_2'=4,'grp'=2] {'blk_2'}, dimensions={0} | all-to-all | bytes 1048576 | tf_op jit(solution)/shard_map/all_to_all | solution.py:23
  323.1 12.3 %all_to_all.172 = f32[32,8,128]{2,1,0:T(8,128)S(1)} all-to-all(f32[32,8,128]{2,1,0:T(8,128)S(1)} %broadcast_in_dim.154), channel_id=1, replica_groups=mesh['blk_0'=4,'blk_1'=8,'blk_2'=4,'grp'=2] {'blk_0','blk_1'}, dimensions={0} | all-to-all | bytes 262144 | tf_op jit(solution)/shard_map/all_to_all | solution.py:23
  335.3 0.8 broadcast_in_dim.155
  336.2 3.5 all-to-all-start.24
  341.5 7.2 %all-to-all-done.24 = f32[4,32,8,128]{3,2,1,0:T(8,128)S(1)} async-done(((f32[4,32,8,128]{3,2,1,0:T(8,128)}), f32[4,32,8,128]{3,2,1,0:T(8,128)S(1)}, u32[]{:S(2)}, u32[]{:S(2)}) %all-to-all-start.24) | async-done | bytes 524320 | tf_op jit(solution)/shard_map/all_to_all | solution.py:23
  349.2 12.9 %all_to_all.173 = f32[32,8,128]{2,1,0:T(8,128)S(1)} all-to-all(f32[32,8,128]{2,1,0:T(8,128)S(1)} %broadcast_in_dim.156), channel_id=1, replica_groups=mesh['blk_0'=4,'blk_1'=8,'blk_2'=4,'grp'=2] {'blk_0','blk_1'}, dimensions={0} | all-to-all | bytes 262144 | tf_op jit(solution)/shard_map/all_to_all | solution.py:23
  362.2 9.3 %all_to_all.174 = f32[4,32,8,128]{3,2,1,0:T(8,128)S(1)} all-to-all(f32[4,32,8,128]{3,2,1,0:T(8,128)S(1)} %broadcast_in_dim.157), channel_id=1, replica_groups=mesh['blk_0'=4,'blk_1'=8,'blk_2'=4,'grp'=2] {'blk_2'}, dimensions={0} | all-to-all | bytes 1048576 | tf_op jit(solution)/shard_map/all_to_all | solution.py:23
  372.0 12.7 %all_to_all.175 = f32[32,8,128]{2,1,0:T(8,128)S(1)} all-to-all(f32[32,8,128]{2,1,0:T(8,128)S(1)} %broadcast_in_dim.159), channel_id=1, replica_groups=mesh['blk_0'=4,'blk_1'=8,'blk_2'=4,'grp'=2] {'blk_0','blk_1'}, dimensions={0} | all-to-all | bytes 262144 | tf_op jit(solution)/shard_map/all_to_all | solution.py:23
  384.7 0.8 broadcast_in_dim.160
  385.5 3.5 all-to-all-start.28
  390.8 5.1 %all-to-all-done.28 = f32[4,32,8,128]{3,2,1,0:T(8,128)S(1)} async-done(((f32[4,32,8,128]{3,2,1,0:T(8,128)}), f32[4,32,8,128]{3,2,1,0:T(8,128)S(1)}, u32[]{:S(2)}, u32[]{:S(2)}) %all-to-all-start.28) | async-done | bytes 524320 | tf_op jit(solution)/shard_map/all_to_all | solution.py:23
  396.5 12.4 %all_to_all.176 = f32[32,8,128]{2,1,0:T(8,128)S(1)} all-to-all(f32[32,8,128]{2,1,0:T(8,128)S(1)} %broadcast_in_dim.161), channel_id=1, replica_groups=mesh['blk_0'=4,'blk_1'=8,'blk_2'=4,'grp'=2] {'blk_0','blk_1'}, dimensions={0} | all-to-all | bytes 262144 | tf_op jit(solution)/shard_map/all_to_all | solution.py:23
  408.9 0.8 broadcast_in_dim.162
  409.7 4.1 all-to-all-start.30
  413.9 2.3 slice.42
  416.2 6.9 %psum.92 = f32[128]{0:T(128)S(1)} all-reduce(f32[128]{0:T(128)S(1)} %get-tuple-element.10), channel_id=1, replica_groups=mesh['blk_0'=4,'blk_1'=8,'blk_2'=4,'grp'=2] {'blk_0'}, use_global_device_ids=true, to_apply=%region_12.0 | all-reduce | flops 128 | bytes 1024 | tf_op jit(solution)/shard_map/psum | solution.py:18
  423.1 11.5 %psum.93 = f32[128]{0:T(128)S(1)} all-reduce(f32[128]{0:T(128)S(1)} %psum.92), channel_id=1, replica_groups=mesh['blk_0'=4,'blk_1'=8,'blk_2'=4,'grp'=2] {'blk_1'}, use_global_device_ids=true, to_apply=%region_13.0 | all-reduce | flops 128 | bytes 1024 | tf_op jit(solution)/shard_map/psum | solution.py:18
  434.6 9.2 %psum.94 = f32[128]{0:T(128)S(1)} all-reduce(f32[128]{0:T(128)S(1)} %psum.93), channel_id=1, replica_groups=mesh['blk_0'=4,'blk_1'=8,'blk_2'=4,'grp'=2] {'blk_2'}, use_global_device_ids=true, to_apply=%region_14.0 | all-reduce | flops 128 | bytes 1024 | tf_op jit(solution)/shard_map/psum | solution.py:18
  443.8 43.7 %psum.95 = f32[128]{0:T(128)S(1)} all-reduce(f32[128]{0:T(128)S(1)} %psum.94), channel_id=1, replica_groups=mesh['blk_0'=4,'blk_1'=8,'blk_2'=4,'grp'=2] {'grp'}, use_global_device_ids=true, to_apply=%region_15.0 | all-reduce | flops 128 | bytes 1024 | tf_op jit(solution)/shard_map/psum | solution.py:18
  487.4 1.2 copy.38
  489.0 0.9 convolution_add_fusion.5
  490.0 1.1 maximum_add_fusion
  (79 shorter events, 7.6 us)
Async XLA Ops:
  0.6 109.6 %copy-start = (f32[8,8,8,1024]{3,2,1,0:T(8,128)S(1)}, f32[8,8,8,1024]{3,2,1,0:T(8,128)}, u32[]{:S(2)}) copy-start(f32[8,8,8,1024]{3,2,1,0:T(8,128)} %param.12) | copy-start | bytes 6291460
  6.5 47.3 %copy-start.6 = (s32[2,24]{1,0:T(2,128)S(1)}, s32[2,24]{1,0:T(2,128)}, u32[]{:S(2)}) copy-start(s32[2,24]{1,0:T(2,128)} %param.10) | copy-start | bytes 580
  6.5 51.9 %copy-start.5 = (s32[8]{0:T(128)S(1)}, s32[8]{0:T(128)}, u32[]{:S(2)}) copy-start(s32[8]{0:T(128)} %param.11) | copy-start | bytes 100
  52.8 1.0 copy-start.2
  52.8 30.9 %copy-start.4 = (f32[8,8,1024]{2,1,0:T(8,128)S(1)}, f32[8,8,1024]{2,1,0:T(8,128)}, u32[]{:S(2)}) copy-start(f32[8,8,1024]{2,1,0:T(8,128)} %param.13) | copy-start | bytes 786436
  54.7 6.2 %all-to-all-start = ((f32[2,8,8,128]{3,2,1,0:T(8,128)}), f32[2,8,8,128]{3,2,1,0:T(8,128)S(1)}, u32[]{:S(2)}, u32[]{:S(2)}) async-start(f32[2,8,8,128]{3,2,1,0:T(8,128)} %broadcast_in_dim.125), calls=%async_computation | async-start | bytes 131072 | tf_op jit(solution)/shard_map/all_to_all | solution.py:23
  99.8 10.4 %all-to-all-start.4 = ((f32[4,32,8,128]{3,2,1,0:T(8,128)}), f32[4,32,8,128]{3,2,1,0:T(8,128)S(1)}, u32[]{:S(2)}, u32[]{:S(2)}) async-start(f32[4,32,8,128]{3,2,1,0:T(8,128)} %broadcast_in_dim.130), calls=%async_computation.4 | async-start | bytes 1048576 | tf_op jit(solution)/shard_map/all_to_all | solution.py:23
  146.6 10.4 %all-to-all-start.8 = ((f32[4,32,8,128]{3,2,1,0:T(8,128)}), f32[4,32,8,128]{3,2,1,0:T(8,128)S(1)}, u32[]{:S(2)}, u32[]{:S(2)}) async-start(f32[4,32,8,128]{3,2,1,0:T(8,128)} %broadcast_in_dim.135), calls=%async_computation.8 | async-start | bytes 1048576 | tf_op jit(solution)/shard_map/all_to_all | solution.py:23
  193.3 10.7 %all-to-all-start.12 = ((f32[4,32,8,128]{3,2,1,0:T(8,128)}), f32[4,32,8,128]{3,2,1,0:T(8,128)S(1)}, u32[]{:S(2)}, u32[]{:S(2)}) async-start(f32[4,32,8,128]{3,2,1,0:T(8,128)} %broadcast_in_dim.140), calls=%async_computation.12 | async-start | bytes 1048576 | tf_op jit(solution)/shard_map/all_to_all | solution.py:23
  240.5 10.4 %all-to-all-start.16 = ((f32[4,32,8,128]{3,2,1,0:T(8,128)}), f32[4,32,8,128]{3,2,1,0:T(8,128)S(1)}, u32[]{:S(2)}, u32[]{:S(2)}) async-start(f32[4,32,8,128]{3,2,1,0:T(8,128)} %broadcast_in_dim.145), calls=%async_computation.16 | async-start | bytes 1048576 | tf_op jit(solution)/shard_map/all_to_all | solution.py:23
  287.2 10.4 %all-to-all-start.20 = ((f32[4,32,8,128]{3,2,1,0:T(8,128)}), f32[4,32,8,128]{3,2,1,0:T(8,128)S(1)}, u32[]{:S(2)}, u32[]{:S(2)}) async-start(f32[4,32,8,128]{3,2,1,0:T(8,128)} %broadcast_in_dim.150), calls=%async_computation.20 | async-start | bytes 1048576 | tf_op jit(solution)/shard_map/all_to_all | solution.py:23
  336.2 12.5 %all-to-all-start.24 = ((f32[4,32,8,128]{3,2,1,0:T(8,128)}), f32[4,32,8,128]{3,2,1,0:T(8,128)S(1)}, u32[]{:S(2)}, u32[]{:S(2)}) async-start(f32[4,32,8,128]{3,2,1,0:T(8,128)} %broadcast_in_dim.155), calls=%async_computation.24 | async-start | bytes 1048576 | tf_op jit(solution)/shard_map/all_to_all | solution.py:23
  385.5 10.4 %all-to-all-start.28 = ((f32[4,32,8,128]{3,2,1,0:T(8,128)}), f32[4,32,8,128]{3,2,1,0:T(8,128)S(1)}, u32[]{:S(2)}, u32[]{:S(2)}) async-start(f32[4,32,8,128]{3,2,1,0:T(8,128)} %broadcast_in_dim.160), calls=%async_computation.28 | async-start | bytes 1048576 | tf_op jit(solution)/shard_map/all_to_all | solution.py:23
  409.7 77.7 %all-to-all-start.30 = ((f32[4,32,8,128]{3,2,1,0:T(8,128)}), f32[4,32,8,128]{3,2,1,0:T(8,128)}, u32[]{:S(2)}, u32[]{:S(2)}) async-start(f32[4,32,8,128]{3,2,1,0:T(8,128)} %broadcast_in_dim.162), calls=%async_computation.30 | async-start | bytes 1048576 | tf_op jit(solution)/shard_map/all_to_all | solution.py:23
  413.9 76.1 %copy-start.1 = (f32[2,1024,128]{2,1,0:T(8,128)S(1)}, f32[2,1024,128]{2,1,0:T(8,128)}, u32[]{:S(2)}) copy-start(f32[2,1024,128]{2,1,0:T(8,128)} %param.9) | copy-start | bytes 3145732
  487.4 2.5 copy-start.3
where the time goes:
time: 493 us; the launch traced here: 491 us
  blocking collectives  376 us (76%)
  waiting for transfers between devices  37.7 us (8%)
  starting transfers between devices  32.1 us (7%)
  between operations  16.1 us (3%)
  local copies, waits for them, and re-layouts  13.7 us (3%)
  matrix products  11.4 us (2%)
    all_to_all x22, blocking collectives, copy_for_each(): return lax.all_to_all(copies, axis, split_axis=0, concat_axis=0, tiled=True)  260 us
    psum x8, blocking collectives, one_axis_at_a_time(): return functools.reduce(lax.psum, axes, shard)  116 us
    all_to_all x9, waiting for transfers between devices, copy_for_each(): return lax.all_to_all(copies, axis, split_axis=0, concat_axis=0, tiled=True)  37.7 us
    all_to_all x9, starting transfers between devices, copy_for_each(): return lax.all_to_all(copies, axis, split_axis=0, concat_axis=0, tiled=True)  32.1 us
  transfers between devices with their start and end apart: 9, of which 7 were waited for; matrix products, arithmetic and copies ran while one was open for 1% of the time, Pallas kernels for 0%

commit v1 on v0

v1 whole, which is shorter than its diff:
```python
import jax
import jax.numpy as jnp
from jax import lax
from jax.experimental import pallas as pl
from jax.experimental.pallas import tpu as pltpu
from jax.sharding import Mesh
from jax.sharding import PartitionSpec as P

PANELS = 8
NY, NZ, NX, NC = 4, 8, 4, 2
BLOCKS = PANELS * (PANELS + 1) // 2
GRAN = 3
NGRAN = BLOCKS // GRAN
COLS = 8
BLK_GRP = ("blk_0", "blk_1", "blk_2", "grp")
BLK = ("blk_0", "blk_1", "blk_2")
MESH = pl.DeviceIdType.MESH
precise = lax.Precision.HIGHEST
f32 = jnp.float32
bf16 = jnp.bfloat16


def f_at(t, u):
    return t * (t + 1) // 2 + u


def d_at(t):
    return t * (t + 1) // 2 + t


BLOCK_OF = [(t, u) for t in range(PANELS) for u in range(t + 1)]


def kernel(
    order, f_ref, d_ref, pk, stat, r_ref, a_ref,
    sol_out, stat_out,
    fp, G, cin, cown, S, sbuf, rbuf, wbuf, opk, sol, stat_s, stat_r,
    st_send, st_recv, rl_send, rl_recv, dd_send, dd_recv,
    rd_send, rd_recv, c_send, c_recv, o_send, o_recv, t_send, t_recv,
):
    y = lax.axis_index("blk_0")
    z = lax.axis_index("blk_1")
    x = lax.axis_index("blk_2")
    c = lax.axis_index("grp")
    q = z * 2 + c
    znext = lax.rem(z + 1 - 2 * c + NZ, NZ)

    def dev(y=y, z=z, x=x, c=c):
        return {"blk_0": y, "blk_1": z, "blk_2": x, "grp": c}

    ypeers = [lax.rem(y + d, NY) for d in range(1, NY)]
    xpeers = [lax.rem(x + d, NX) for d in range(1, NX)]
    zcpeers = [
        (lax.rem(z + dz, NZ), lax.rem(c + dc, NC))
        for dz in range(NZ) for dc in range(NC) if dz or dc
    ]

    barrier = pltpu.get_barrier_semaphore()
    for p in ypeers:
        pl.semaphore_signal(barrier, inc=1, device_id=dev(y=p), device_id_type=MESH)
    for p in xpeers:
        pl.semaphore_signal(barrier, inc=1, device_id=dev(x=p), device_id_type=MESH)
    for pz, pc in zcpeers:
        pl.semaphore_signal(barrier, inc=1, device_id=dev(z=pz, c=pc), device_id_type=MESH)

    group = lax.broadcasted_iota(jnp.int32, (8, 128), 1) // 8 % 4
    for b, (t, u) in enumerate(BLOCK_OF):
        if u < t:
            row = f_ref[order[t] * PANELS + order[u]]
            for s in range(NY):
                fp[b, s] = row[:, 256 * s : 256 * s + 256]
        else:
            row = d_ref[order[t]]
            for s in range(NX):
                for zh in range(2):
                    piece = jnp.zeros((8, 128), f32)
                    for yy in range(NY):
                        nat = row[:, yy * 256 + zh * 128 : yy * 256 + zh * 128 + 128]
                        shift = (8 * (yy - s)) % 128
                        if shift:
                            nat = pltpu.roll(nat, shift, 1)
                        piece = jnp.where(group == yy, nat, piece)
                    fp[b, s, :, zh * 128 : zh * 128 + 128] = piece

    pl.semaphore_wait(barrier, len(ypeers) + len(xpeers) + len(zcpeers))

    def rcopy(src, dst, ss, rs, to):
        return pltpu.make_async_remote_copy(
            src_ref=src, dst_ref=dst, send_sem=ss, recv_sem=rs, device_id=to, device_id_type=MESH
        )

    me = dev(x=xpeers[0])

    def wait_recv(ref, sem):
        rcopy(ref, ref, sem, sem, me).wait_recv()

    def wait_send(ref, sem):
        rcopy(ref, ref, sem, sem, me).wait_send()

    for pz, pc in zcpeers:
        rcopy(pk.at[pz * 2 + pc], cin.at[q], c_send.at[0], c_recv.at[0], dev(z=pz, c=pc)).start()
    cin[q] = pk[q]

    def stage(g):
        for b in range(g * GRAN, g * GRAN + GRAN):
            t, u = BLOCK_OF[b]
            if u < t:
                G[b, z, y] = fp[b, y]
                for p in ypeers:
                    rcopy(fp.at[b, p], G.at[b, z, y], st_send.at[g], st_recv.at[g], dev(y=p)).start()
            else:
                G[b, z, x] = fp[b, x]
                for p in xpeers:
                    rcopy(fp.at[b, p], G.at[b, z, x], st_send.at[g], st_recv.at[g], dev(x=p)).start()

    def piece(g, h):
        zo = lax.rem(z - h * (1 - 2 * c) + NZ, NZ)
        if h == 4:
            return G.at[pl.ds(g * GRAN, GRAN), zo, pl.ds(2 * c, 2)]
        return G.at[pl.ds(g * GRAN, GRAN), zo]

    def send(g, h):
        ref = piece(g, h - 1)
        if h == 4:
            zo = lax.rem(z - 3 * (1 - 2 * c) + NZ, NZ)
            ref = G.at[pl.ds(g * GRAN, GRAN), zo, pl.ds(2 * c, 2)]
        rcopy(ref, ref, rl_send.at[g, h - 1], rl_recv.at[g, h - 1], dev(z=znext)).start()

    def share(g, h):
        ref = piece(g, h)
        rcopy(ref, ref, dd_send.at[g, h - 1], dd_recv.at[g, h - 1], dev(c=1 - c)).start()

    done = {"stage": 0, "slot": 0, "gran": 0}

    def stage_upto(n):
        while done["stage"] < min(n, NGRAN):
            stage(done["stage"])
            done["stage"] += 1

    def slots_upto(n):
        while done["slot"] < min(n, NGRAN + 4):
            k = done["slot"]
            stage_upto(k + 3)
            for h in range(4, -1, -1):
                g = k - h
                if not 0 <= g < NGRAN:
                    continue
                if h == 0:
                    wait_recv(fp.at[pl.ds(0, 3 * GRAN), 0], st_recv.at[g])
                    send(g, 1)
                else:
                    wait_recv(piece(g, h), rl_recv.at[g, h - 1])
                    if h < 4:
                        send(g, h + 1)
                    share(g, h)
            done["slot"] += 1

    def granules_upto(b):
        while done["gran"] * GRAN <= b:
            g = done["gran"]
            slots_upto(g + 5)
            for h in range(1, 5):
                zo = lax.rem(z + h * (1 - 2 * c) + NZ, NZ)
                ref = G.at[pl.ds(g * GRAN, GRAN), zo]
                if h == 4:
                    ref = G.at[pl.ds(g * GRAN, GRAN), zo, pl.ds(2 - 2 * c, 2)]
                wait_recv(ref, dd_recv.at[g, h - 1])
            done["gran"] += 1

    def product(v, b):
        block = G[b].reshape(256, 256)
        high = block.astype(bf16)
        low = (block - high.astype(f32)).astype(bf16)
        v_high = v.astype(bf16)
        v_low = (v - v_high.astype(f32)).astype(bf16)
        both = jnp.concatenate([v_high, v_low], axis=0)
        dims = (((1,), (1,)), ((), ()))
        first = lax.dot_general(both, high, dims, preferred_element_type=f32)
        second = lax.dot_general(v_high, low, dims, preferred_element_type=f32)
        return first[:16] + first[16:] + second

    def peers_of(phase):
        return [
            [dev(c=1 - c)],
            [dev(x=p) for p in xpeers],
            [dev(y=p) for p in ypeers],
            [dev(z=lax.rem(z + d, NZ)) for d in range(1, NZ)],
        ][phase % 4]

    def stat_send(phase):
        for d, to in enumerate(peers_of(phase)):
            rcopy(stat_s.at[phase], stat_r.at[phase, d], t_send.at[phase], t_recv.at[phase], to).start()

    def stat_take(phase):
        n = len(peers_of(phase))
        wait_recv(stat_r.at[phase, pl.ds(0, n)], t_recv.at[phase])
        total = stat_s[phase]
        for d in range(n):
            total = total + stat_r[phase, d]
        return total

    def stat_tick(tick):
        if tick == 0:
            stat_s[0] = stat[...]
            stat_send(0)
        elif tick < 8:
            total = stat_take(tick - 1)
            if tick == 4:
                stat_out[0] = total
                step = total[0:1] / total[1:2]

                def body(i, acc):
                    at = pl.ds(pl.multiple_of(i * 128, 128), 128)
                    new = r_ref[at, :] - step * a_ref[at, :]
                    return acc + jnp.sum((new * new).reshape(16, 8, 128), axis=0)

                acc = lax.fori_loop(0, 16, body, jnp.zeros((8, 128), f32))
                total = jnp.broadcast_to(jnp.sum(acc, axis=0, keepdims=True), (8, 128))
            stat_s[tick] = total
            stat_send(tick)
        elif tick == 8:
            stat_out[1] = stat_take(7)

    def exchange(tick, value, targets):
        sbuf[tick] = value
        for d, to in enumerate(targets):
            rcopy(sbuf.at[tick], rbuf.at[tick, d], rd_send.at[tick], rd_recv.at[tick], to).start()

    def finish(tick):
        wait_recv(rbuf.at[tick], rd_recv.at[tick])
        return (sbuf[tick] + rbuf[tick, 0]) + (rbuf[tick, 1] + rbuf[tick, 2])

    stage_upto(3)
    slots_upto(2)

    wait_recv(cin.at[pl.ds(0, NZ * NC - 1)], c_recv.at[0])
    lane = lax.broadcasted_iota(jnp.int32, (8, 128), 1)
    quads = [cin[2 * zz] + cin[2 * zz + 1] for zz in range(NZ)]

    def own(k, t):
        halves = []
        for zh in range(2):
            acc = jnp.zeros((8, 128), f32)
            for zl in range(4):
                src = quads[zh * 4 + zl]
                shift = (zl * 32 - (k * 64 + t * 8)) % 128
                if shift:
                    src = pltpu.roll(src, shift, 1)
                acc = jnp.where((lane >= zl * 32) & (lane < zl * 32 + 8), src, acc)
            halves.append(pltpu.roll(acc, y * 8, 1))
        return halves

    for t in range(PANELS):
        for k in range(2):
            for zh, half in enumerate(own(k, t)):
                cown[t, k * 8 : k * 8 + 8, zh * 128 : zh * 128 + 128] = half

    pending = cown[0]
    for t in range(PANELS):
        tick = 2 * t
        if t:
            pending = pending - product(S[t - 1], f_at(t, t - 1))
        exchange(tick, pending, [dev(y=p) for p in ypeers])
        stat_tick(tick)
        slots_upto(tick + 3)
        granules_upto(d_at(t))
        target = finish(tick)

        tick += 1
        exchange(tick, product(target, d_at(t)), [dev(x=p) for p in xpeers])
        stat_tick(tick)
        slots_upto(tick + 3)
        if t + 1 < PANELS:
            granules_upto(f_at(t + 1, t))
            pending = cown[t + 1]
            for u in range(t):
                pending = pending - product(S[u], f_at(t + 1, u))
        S[t] = finish(tick)
        back = lax.rem(128 - 8 * x, 128)
        for k in range(2):
            for zh in range(2):
                wbuf[t, k, zh] = pltpu.roll(S[t, k * 8 : k * 8 + 8, zh * 128 : zh * 128 + 128], back, 1)

    for zz in range(NZ):
        acc = jnp.zeros((8, 128), f32)
        for t in range(PANELS):
            for k in range(2):
                src = wbuf[t, k, zz // 4]
                shift = (k * 64 + t * 8 - (zz % 4) * 32) % 128
                if shift:
                    src = pltpu.roll(src, shift, 1)
                at = k * 64 + t * 8
                acc = jnp.where((lane >= at) & (lane < at + 8), src, acc)
        opk[zz] = acc
    for pz, pc in zcpeers:
        rcopy(opk.at[pz], sol.at[q], o_send.at[0], o_recv.at[0], dev(z=pz, c=pc)).start()
    sol[q] = opk[z]
    wait_recv(sol.at[pl.ds(0, NZ * NC - 1)], o_recv.at[0])
    sol_out[...] = sol[...]

    wait_send(cin.at[pl.ds(0, NZ * NC - 1)], c_send.at[0])
    wait_send(sol.at[pl.ds(0, NZ * NC - 1)], o_send.at[0])
    for g in range(NGRAN):
        wait_send(fp.at[pl.ds(0, 3 * GRAN), 0], st_send.at[g])
        for h in range(1, 5):
            wait_send(piece(g, h), rl_send.at[g, h - 1])
            wait_send(piece(g, h), dd_send.at[g, h - 1])
    for tick in range(2 * PANELS):
        wait_send(rbuf.at[tick], rd_send.at[tick])
    for phase in range(8):
        wait_send(stat_r.at[phase, pl.ds(0, len(peers_of(phase)))], t_send.at[phase])


def coarse_kernel(order, f_own, d_own, pk, stat, r, a):
    vmem = pl.BlockSpec(memory_space=pltpu.VMEM)
    smem = pl.BlockSpec(memory_space=pltpu.SMEM)
    dma = pltpu.SemaphoreType.DMA
    return pl.pallas_call(
        kernel,
        out_shape=(
            jax.ShapeDtypeStruct((16, 8, 128), f32),
            jax.ShapeDtypeStruct((2, 8, 128), f32),
        ),
        in_specs=[smem] + [vmem] * 6,
        out_specs=(vmem, vmem),
        scratch_shapes=[
            pltpu.VMEM((BLOCKS, 4, 8, 256), f32),
            pltpu.VMEM((BLOCKS, NZ, 4, 8, 256), f32),
            pltpu.VMEM((16, 8, 128), f32),
            pltpu.VMEM((PANELS, 16, 256), f32),
            pltpu.VMEM((PANELS, 16, 256), f32),
            pltpu.VMEM((2 * PANELS, 16, 256), f32),
            pltpu.VMEM((2 * PANELS, 3, 16, 256), f32),
            pltpu.VMEM((PANELS, 2, 2, 8, 128), f32),
            pltpu.VMEM((NZ, 8, 128), f32),
            pltpu.VMEM((16, 8, 128), f32),
            pltpu.VMEM((8, 8, 128), f32),
            pltpu.VMEM((8, 7, 8, 128), f32),
            dma((NGRAN,)), dma((NGRAN,)),
            dma((NGRAN, 4)), dma((NGRAN, 4)),
            dma((NGRAN, 4)), dma((NGRAN, 4)),
            dma((2 * PANELS,)), dma((2 * PANELS,)),
            dma((1,)), dma((1,)),
            dma((1,)), dma((1,)),
            dma((8,)), dma((8,)),
        ],
        compiler_params=pltpu.CompilerParams(
            collective_id=0, has_side_effects=True, vmem_limit_bytes=40 * 1024 * 1024
        ),
    )(order, f_own, d_own, pk, stat, r, a)


def local(
    schur_blocks, residual, direction, corner_map, panel_order, coarse_factor, block_inverses
):
    sub_count, rows, columns = residual.shape
    corners = corner_map.shape[1]
    position = jnp.zeros((PANELS,), jnp.int32).at[panel_order].set(jnp.arange(PANELS, dtype=jnp.int32))
    hot = (corner_map[:, :, None] // 8 == jnp.arange(PANELS, dtype=jnp.int32)).astype(jnp.int32)
    slot = jnp.sum(hot * position, axis=-1) * 8 + corner_map % 8
    placing = (slot[:, :, None] == lax.broadcasted_iota(jnp.int32, (1, 1, 64), 2)).astype(f32)
    applied = jnp.einsum(
        "sij,sjv->siv", schur_blocks, direction.astype(bf16), preferred_element_type=f32
    )
    rr = jnp.sum(residual * residual, axis=(0, 1))
    curvature = jnp.sum(direction * applied, axis=(0, 1))
    stat = jnp.concatenate([rr[None], curvature[None], jnp.zeros((6, columns), f32)], axis=0)
    pk_r = jnp.einsum("scm,scv->vm", placing, residual[:, :corners], precision=precise)
    pk_a = jnp.einsum("scm,scv->vm", placing, applied[:, :corners], precision=precise)
    pk = jnp.concatenate([pk_r, pk_a], axis=1).reshape(16, 8, 128)
    sol, stats = coarse_kernel(
        panel_order,
        coarse_factor.reshape(PANELS * PANELS, 8, 1024),
        block_inverses,
        pk,
        stat,
        residual.reshape(-1, columns),
        applied.reshape(-1, columns),
    )
    norm_now = stats[0, 0]
    step = norm_now / stats[0, 1]
    norm_next = stats[1, 0]
    flat = sol.reshape(columns, 128)
    solved = flat[:, :64] - step[:, None] * flat[:, 64:]
    residual = residual - step * applied
    correction = jnp.einsum("scm,vm->scv", placing, solved, precision=precise)
    corrected = jnp.concatenate(
        [residual[:, :corners] + correction, residual[:, corners:]], axis=1
    )
    direction = corrected + norm_next / norm_now * direction
    return residual, direction


def solution(mesh):
    split = Mesh(
        mesh.devices.reshape(NY, NZ, NX, NC), ("blk_0", "blk_1", "blk_2", "grp")
    )
    placed = (
        P(BLK_GRP, None, None),
        P(BLK_GRP, None, None),
        P(BLK_GRP, None, None),
        P(BLK_GRP, None),
        P(),
        P(None, None, BLK, None),
        P(None, BLK, None),
    )
    return jax.shard_map(
        local,
        mesh=split,
        in_specs=placed,
        out_specs=(P(BLK_GRP, None, None), P(BLK_GRP, None, None)),
        check_vma=False,
    )
```

time: 493 us -> 123 us (0.25)
  blocking collectives: 376 us -> 0 us
  Pallas kernels: 0 us -> 105 us
  waiting for transfers between devices: 37.7 us -> 0 us
  starting transfers between devices: 32.1 us -> 0 us
  between operations: 16.1 us -> 0.76 us
  local copies, waits for them, and re-layouts: 13.7 us -> 3.89 us
  matrix products: 11.4 us -> 6.45 us
    all_to_all x22 -> x0, blocking collectives: 260 us -> none  [copy_for_each(): return lax.all_to_all(copies, axis, split_axis=0, concat_axis=0, tiled=True)]
    psum x8 -> x0, blocking collectives: 116 us -> none  [one_axis_at_a_time(): return functools.reduce(lax.psum, axes, shard)]
    pallas_call x0 -> x1, Pallas kernels: none -> 105 us  [coarse_kernel(): pl.pallas_call(kernel, out_shape=(jax.ShapeDtypeStruct((16, 8, 128), f32)...]
    all_to_all x9 -> x0, waiting for transfers between devices: 37.7 us -> none  [copy_for_each(): return lax.all_to_all(copies, axis, split_axis=0, concat_axis=0, tiled=True)]
    all_to_all x9 -> x0, starting transfers between devices: 32.1 us -> none  [copy_for_each(): return lax.all_to_all(copies, axis, split_axis=0, concat_axis=0, tiled=True)]
    broadcast_in_dim x32 -> x1, local copies, waits for them, and re-layouts: 7.72 us -> 0.01 us  [local(): jnp.zeros((6, columns), f32)]
    dot_general x18 -> x4, matrix products: 11.4 us -> 6.45 us  [the longest x1 4.18 us: local(): jnp.einsum('sij,sjv->siv', schur_blocks, direction.astype(bf16), preferre...]
  transfers between devices with their start and end apart: 9 -> 0, of which waited for: 7 -> 0; matrix products, arithmetic and copies ran while one was open for 1% -> 0% of each run, Pallas kernels for 0% -> 0%
where the time goes in v1:
time: 123 us; the launch traced here: 122 us
  Pallas kernels  105 us (85%)
  matrix products  6.45 us (5%)
  other arithmetic  6.07 us (5%)
  local copies, waits for them, and re-layouts  3.89 us (3%)
    pallas_call x1, Pallas kernels, coarse_kernel(): pl.pallas_call(kernel, out_shape=(jax.ShapeDtypeStruct((16, 8, 128), f32)...  105 us
    dot_general x1, matrix products, local(): jnp.einsum('sij,sjv->siv', schur_blocks, direction.astype(bf16), preferre...  4.18 us

profile of v1, /device:TPU:1, one launch (start us, length us, event | category | flops | bytes accessed | tf_op | source)
XLA Modules:
  0.0 122.2 jit_solution(17646714452216649156)
XLA Ops:
  0.6 0.0 copy-start
  0.6 0.0 copy-start.3
  0.7 0.0 copy-start.2
  0.7 0.8 compare_select_fusion
  1.4 1.5 %multiply_reduce_fusion.1 = f32[128]{0:T(128)S(1)} fusion(f32[2,1024,128]{2,1,0:T(8,128)} %param.8), kind=kLoop, calls=%fused_computation.7 | loop fusion | flops 524160 | bytes 1049088 | tf_op jit(solution)/shard_map/reduce_sum | solution.py:365
  2.9 0.1 pad.4.clone
  3.0 0.6 scatter_custom_fusion
  3.6 0.7 and_select_fusion.1
  4.3 0.1 select_reduce_fusion
  4.4 0.7 fusion.11
  5.1 1.0 convolution_bitcast_fusion.1
  6.1 4.2 %multiply_reduce_fusion = (f32[128]{0:T(128)S(1)}, f32[2,1024,128]{2,1,0:T(8,128)S(1)}) fusion(f32[2,1024,128]{2,1,0:T(8,128)} %param.9, bf16[2,1024,1024]{2,1,0:T(8,128)(2,1)} %param.7), kind=kOutput, calls=%fused_computation.6 | convolution fusion | flops 537657216 | bytes 6291968 | tf_op jit(solution)/shard_map/sij,sjv->siv/dot_general | solution.py:362
  10.3 0.1 maximum_maximum_fusion.stat
  10.4 0.3 convolution_bitcast_fusion
  10.7 0.1 copy.12
  10.8 0.0 copy-done
  10.8 0.0 copy-done.3
  10.8 0.0 copy-done.2
  10.8 0.0 copy-start.1
  10.8 1.6 %copy-done.1 = f32[8,8,8,1024]{3,2,1,0:T(8,128)S(1)} copy-done((f32[8,8,8,1024]{3,2,1,0:T(8,128)S(1)}, f32[8,8,8,1024]{3,2,1,0:T(8,128)}, u32[]{:S(2)}) %copy-start.1) | copy-done | bytes 2097176
  12.4 0.0 copy-start.4
  12.4 105.0 %shard_map.86 = (f32[16,8,128]{2,1,0:T(8,128)S(1)}, f32[2,8,128]{2,1,0:T(8,128)S(1)}) custom-call(s32[8]{0:T(128)S(1)} %copy-done.3, f32[64,8,1024]{2,1,0:T(8,128)S(1)} %bitcast.24, f32[8,8,1024]{2,1,0:T(8,128)S(1)} %copy-done.2, f32[16,8,128]{2,1,0:T(8,128)S(1)} %bitcast.25, f32[8,128]{1,0:T(8,128)S(1)} %maximum_maximum_fusion.stat, ...), custom_call_target="tpu_custom_call" | custom-call | tf_op jit(solution)/shard_map/pallas_call | solution.py:318
  117.4 1.1 multiply_subtract_fusion
  118.5 0.1 fusion.16
  118.6 0.1 copy.16
  118.7 0.1 copy.15
  118.8 1.0 convolution_add_fusion
  119.7 1.3 %slice.40 = f32[2,1000,128]{2,1,0:T(8,128)S(1)} slice(f32[2,1024,128]{2,1,0:T(8,128)} %multiply_subtract_fusion), slice={[0:2], [24:1024], [0:128]} | slice | bytes 2048000 | tf_op jit(solution)/shard_map/slice | solution.py:388
  121.0 0.0 copy-done.4
  121.0 1.1 maximum_add_fusion
  (4 shorter events, 0.0 us)
Async XLA Ops:
  0.6 10.1 %copy-start = (f32[2,1024,128]{2,1,0:T(8,128)S(1)}, f32[2,1024,128]{2,1,0:T(8,128)}, u32[]{:S(2)}) copy-start(f32[2,1024,128]{2,1,0:T(8,128)} %param.8) | copy-start | bytes 3145732
  0.6 10.1 %copy-start.3 = (s32[8]{0:T(128)S(1)}, s32[8]{0:T(128)}, u32[]{:S(2)}) copy-start(s32[8]{0:T(128)} %order.1) | copy-start | bytes 100
  0.7 10.1 %copy-start.2 = (f32[8,8,1024]{2,1,0:T(8,128)S(1)}, f32[8,8,1024]{2,1,0:T(8,128)}, u32[]{:S(2)}) copy-start(f32[8,8,1024]{2,1,0:T(8,128)} %d_ref.1) | copy-start | bytes 786436
  10.8 1.6 %copy-start.1 = (f32[8,8,8,1024]{3,2,1,0:T(8,128)S(1)}, f32[8,8,8,1024]{3,2,1,0:T(8,128)}, u32[]{:S(2)}) copy-start(f32[8,8,8,1024]{3,2,1,0:T(8,128)} %param.12) | copy-start | bytes 6291460
  12.4 108.6 %copy-start.4 = (f32[2,1024,128]{2,1,0:T(8,128)S(1)}, f32[2,1024,128]{2,1,0:T(8,128)}, u32[]{:S(2)}) copy-start(f32[2,1024,128]{2,1,0:T(8,128)} %param.9) | copy-start | bytes 3145732
